TPU v7x, 256 devices: a whole 4x4x8 slice. The times are simulated.
256 devices in a mesh: batch: 128 (over x_hi, y, z, core), rep: 2 (over x_lo).
Axes of the slice: x: 4 (x_hi: 2, x_lo: 2; x = x_hi * 2 + x_lo), y: 4, z: 8, core: 2. Of those that a mesh axis runs over, the one named last changes fastest.
Arguments:
- image_embed: bfloat16 [16384, 1024], P('batch'), may hold values from -2 to 2
- text_embed: bfloat16 [16384, 1024], P(('batch', 'rep')), may hold values from -2 to 2
- logit_scale: float32 [1], replicated, may hold values from 50 to 100
Outputs:
- mean_loss: float32 [], replicated
- image_grad: float32 [16384, 1024], P(('batch', 'rep'))
- text_grad: float32 [16384, 1024], P(('batch', 'rep'))
All inputs are finite; a program needn't handle non-finite values.
Results may differ from a plain program's by a relative error of at most 0.0025.
Values may be sent and summed in bfloat16 or wider, within the bound.
No kernel may reach another device: no remote copies, remote signals or barrier semaphores. Data moves between devices by JAX's collectives and lax.ppermute only.
A program may use at most 128 MiB of HBM per device.

v0:
```python
import functools
import jax
import jax.numpy as jnp
from jax import lax
from jax.sharding import Mesh
from jax.sharding import PartitionSpec as P

BATCH = ("batch_0", "batch_1", "batch_2", "batch_3")
BATCH_REP = ("batch_0", "batch_1", "batch_2", "batch_3", "rep")


def copy_for_each(array, axis):
    peers = lax.axis_size(axis)
    return lax.all_to_all(
        jnp.broadcast_to(array[None], (peers, *array.shape)), axis, 0, 0, tiled=True
    )


def all_in_one(array, axis):
    leaves = jax.tree.leaves(array)
    sequence = sorted(range(len(leaves)), key=lambda k: -leaves[k].size)
    width = (1, *leaves[sequence[0]].shape)[-1]
    lines = [
        jnp.pad(leaves[k].reshape(-1), (0, -leaves[k].size % width)).reshape(-1, width)
        for k in sequence
    ]
    both, at, found = (copy_for_each(jnp.concatenate(lines), axis), 0, {})
    for k, line in zip(sequence, lines):
        share = both[:, at : at + len(line)].reshape(len(both), -1)
        found[k] = share[:, : leaves[k].size].reshape(-1, *leaves[k].shape)
        at += len(line)
    numbers = iter(range(len(leaves)))
    return jax.tree.map(lambda _: found[next(numbers)], array)


def joined_by_halves(pieces, combine):
    while len(jax.tree.leaves(pieces)[0]) > 1:
        pieces = jax.vmap(combine)(
            *(jax.tree.map(lambda part: part[side::2], pieces) for side in (0, 1))
        )
    return jax.tree.map(lambda part: part[0], pieces)


def merged(array, axis, combine):
    pieces = all_in_one(array, axis)
    return joined_by_halves(pieces, combine)


def collected_together(array, axis):
    leaves = jax.tree.leaves(array)
    sequence = sorted(range(len(leaves)), key=lambda k: -leaves[k].size)
    width = (1, *leaves[sequence[0]].shape)[-1]
    lines = [
        jnp.pad(leaves[k].reshape(-1), (0, -leaves[k].size % width)).reshape(-1, width)
        for k in sequence
    ]
    both, at, found = (lax.all_gather(jnp.concatenate(lines), axis), 0, {})
    for k, line in zip(sequence, lines):
        share = both[:, at : at + len(line)].reshape(len(both), -1)
        found[k] = share[:, : leaves[k].size].reshape(-1, *leaves[k].shape)
        at += len(line)
    numbers = iter(range(len(leaves)))
    return jax.tree.map(lambda _: found[next(numbers)], array)


def merged_by_axis(array, axes, combine):
    for axis in axes:
        pieces = collected_together(array, axis)
        array = jax.tree.map(lambda part: part[0], pieces)
        for k in range(1, lax.axis_size(axis)):
            array = combine(array, jax.tree.map(lambda part: part[k], pieces))
    return array


def over_axes(array, axes):
    return functools.reduce(lax.psum, axes, array)


def cut_along(array, dim, peers):
    lengths = array.shape
    parts = array.reshape(*lengths[:dim], peers, lengths[dim] // peers, *lengths[dim + 1 :])
    return jnp.moveaxis(parts, dim, 0)


def sum_at_owner(array, axis, dim):
    parts = cut_along(array, dim, lax.axis_size(axis))
    arrived = lax.all_to_all(parts, axis, split_axis=0, concat_axis=0, tiled=True)
    return arrived.sum(axis=0)


def combine_lse(earlier, later):
    biggest = jnp.maximum(earlier[0], later[0])
    return (
        biggest,
        earlier[1] * jnp.exp(earlier[0] - biggest) + later[1] * jnp.exp(later[0] - biggest),
    )


def body(image_embed, text_embed, logit_scale):
    scale_value = logit_scale[0]
    row_count = image_embed.shape[0]
    half_rows = text_embed.shape[0]
    batch_count = lax.axis_size(BATCH)
    batch_index = lax.axis_index(BATCH)
    rep_index = lax.axis_index("rep")
    whole_text = lax.all_gather(text_embed, BATCH, axis=0, tiled=True)
    scores = scale_value * lax.dot_general(
        image_embed, whole_text, (((1,), (1,)), ((), ())), preferred_element_type=jnp.float32
    )
    row_max = jnp.max(scores, axis=1)
    row_sum = jnp.sum(jnp.exp(scores - row_max[:, None]), axis=1)
    row_max, row_sum = merged((row_max, row_sum), "rep", combine_lse)
    row_lse = row_max + jnp.log(row_sum)
    column_max = jnp.max(scores, axis=0)
    column_sum = jnp.sum(jnp.exp(scores - column_max[None, :]), axis=0)
    column_max, column_sum = merged_by_axis((column_max, column_sum), BATCH, combine_lse)
    col_lse = column_max + jnp.log(column_sum)
    own_lse = lax.dynamic_slice_in_dim(col_lse, batch_index * half_rows, half_rows, 0)
    own_scores = lax.dynamic_slice(
        scores, (rep_index * half_rows, batch_index * half_rows), (half_rows, half_rows)
    )
    own_diag = jnp.diagonal(own_scores)
    own_rows = lax.dynamic_slice_in_dim(row_lse, rep_index * half_rows, half_rows, 0)
    loss_sum = over_axes(jnp.sum(own_rows + own_lse - 2.0 * own_diag), BATCH_REP)
    mean_loss = loss_sum / (2 * row_count * batch_count)
    row_ids = lax.broadcasted_iota(jnp.int32, scores.shape, 0) - rep_index * half_rows
    column_ids = lax.broadcasted_iota(jnp.int32, scores.shape, 1) - batch_index * half_rows
    diag_match = ((row_ids == column_ids) & (column_ids >= 0) & (column_ids < half_rows)).astype(
        jnp.float32
    )
    weights = (
        jnp.exp(scores - row_lse[:, None]) + jnp.exp(scores - col_lse[None, :]) - 2.0 * diag_match
    ).astype(jnp.bfloat16)
    image_part = (
        scale_value * 0.5 * jnp.dot(weights, whole_text, preferred_element_type=jnp.float32)
    )
    image_grad = sum_at_owner(image_part, "rep", 0)
    all_rows_lse = lax.all_gather(row_lse, BATCH, axis=0, tiled=True)
    own_first = (2 * batch_index + rep_index) * half_rows
    fragment = lax.all_gather(image_embed, BATCH, axis=0, tiled=True)
    scores_back = scale_value * lax.dot_general(
        text_embed, fragment, (((1,), (1,)), ((), ())), preferred_element_type=jnp.float32
    )
    image_ids = lax.broadcasted_iota(jnp.int32, scores_back.shape, 1)
    text_ids = own_first + lax.broadcasted_iota(jnp.int32, scores_back.shape, 0)
    back_match = (image_ids == text_ids).astype(jnp.float32)
    weights_block = (
        jnp.exp(scores_back - own_lse[:, None])
        + jnp.exp(scores_back - all_rows_lse[None, :])
        - 2.0 * back_match
    ).astype(jnp.bfloat16)
    summed = jnp.dot(weights_block, fragment, preferred_element_type=jnp.float32)
    text_grad = scale_value * 0.5 * summed
    return (mean_loss, image_grad, text_grad)


def solution(mesh):
    split = Mesh(
        mesh.devices.reshape(2, 4, 8, 2, mesh.shape["rep"]),
        ("batch_0", "batch_1", "batch_2", "batch_3", "rep"),
    )
    placed = (P(BATCH, None), P(BATCH_REP, None), P())
    return jax.shard_map(
        body,
        mesh=split,
        in_specs=placed,
        out_specs=(P(), P(BATCH_REP, None), P(BATCH_REP, None)),
        check_vma=False,
    )
```

profile of v0, /device:TPU:1, one launch (start us, length us, event | category | flops | bytes accessed | tf_op | source)
XLA Modules:
  0.0 527.8 jit_solution(11438516798877127760)
XLA Ops:
  7.2 0.7 all-gather.12.cloned.1.call-update
  7.9 0.7 all-gather.14.cloned.1.call-update
  9.4 157.7 %all-gather.12.cloned.1.call-done = bf16[8192,1024]{1,0:T(8,128)(2,1)} async-done(((bf16[64,1024]{1,0:T(8,128)(2,1)}), bf16[8192,1024]{1,0:T(8,128)(2,1)}) %all-gather.12.cloned.1.call-update) | async-done | bytes 16777232 | tf_op jit(solution)/shard_map/all_gather | solution.py:106
  167.1 13.5 %fusion.72 = (f32[128]{0:T(128)S(1)}, f32[8192]{0:T(1024)S(1)}, f32[128,8192]{1,0:T(8,128)}) fusion(bf16[128,1024]{1,0:T(8,128)(2,1)} %param.3, bf16[8192,1024]{1,0:T(8,128)(2,1)} %all-gather.12.cloned.1.call-done, f32[]{:T(128)} %bitcast.315), kind=kOutput, calls=%fused_computation.126 | convolution fusion | flops 2150621184 | bytes 21266948 | tf_op jit(solution)/shard_map/dot_general | solution.py:107
  180.7 3.6 exponential_reduce_fusion.1
  184.2 0.6 broadcast_in_dim.4
  184.8 3.2 all-to-all-start
  188.1 0.1 maximum_bitcast_fusion
  188.1 5.3 %all-gather.4 = f32[2,2,8192]{2,1,0:T(2,128)S(1)} all-gather(f32[1,2,8192]{2,1,0:T(2,128)S(1)} %maximum_bitcast_fusion), channel_id=2, replica_groups=mesh['batch_0'=2,'batch_1'=4,'batch_2'=8,'batch_3'=2,'rep'=2] {'batch_0'}, dimensions={0}, use_global_device_ids=true | all-gather | bytes 196608 | tf_op jit(solution)/shard_map/all_gather | solution.py:57
  193.4 0.1 fusion.47
  193.5 0.1 maximum_bitcast_fusion.1
  193.6 11.0 %all-gather.5 = f32[4,2,8192]{2,1,0:T(2,128)S(1)} all-gather(f32[1,2,8192]{2,1,0:T(2,128)S(1)} %maximum_bitcast_fusion.1), channel_id=3, replica_groups=mesh['batch_0'=2,'batch_1'=4,'batch_2'=8,'batch_3'=2,'rep'=2] {'batch_1'}, dimensions={0}, use_global_device_ids=true | all-gather | bytes 327680 | tf_op jit(solution)/shard_map/all_gather | solution.py:57
  204.6 0.3 fusion.38
  204.9 0.1 maximum_bitcast_fusion.2
  205.0 21.2 %all-gather.6 = f32[8,2,8192]{2,1,0:T(2,128)S(1)} all-gather(f32[1,2,8192]{2,1,0:T(2,128)S(1)} %maximum_bitcast_fusion.2), channel_id=4, replica_groups=mesh['batch_0'=2,'batch_1'=4,'batch_2'=8,'batch_3'=2,'rep'=2] {'batch_2'}, dimensions={0}, use_global_device_ids=true | all-gather | bytes 589824 | tf_op jit(solution)/shard_map/all_gather | solution.py:57
  226.2 0.7 fusion.17
  226.9 0.1 maximum_bitcast_fusion.3
  227.0 9.8 %all-gather.7 = f32[2,2,8192]{2,1,0:T(2,128)S(1)} all-gather(f32[1,2,8192]{2,1,0:T(2,128)S(1)} %maximum_bitcast_fusion.3), channel_id=5, replica_groups=mesh['batch_0'=2,'batch_1'=4,'batch_2'=8,'batch_3'=2,'rep'=2] {'batch_3'}, dimensions={0}, use_global_device_ids=true | all-gather | bytes 196608 | tf_op jit(solution)/shard_map/all_gather | solution.py:57
  236.8 0.1 fusion.76
  236.9 0.8 dynamic_slice.11
  237.8 0.8 gather_fusion
  238.6 0.7 subtract_reduce_fusion
  239.3 5.9 %psum.35 = f32[]{:T(128)} all-reduce(f32[]{:T(128)} %get-tuple-element.7), channel_id=1, replica_groups=mesh['batch_0'=2,'batch_1'=4,'batch_2'=8,'batch_3'=2,'rep'=2] {'batch_0'}, use_global_device_ids=true, to_apply=%region_5.6 | all-reduce | flops 1 | bytes 8 | tf_op jit(solution)/shard_map/psum | solution.py:76
  245.2 9.5 %psum.36 = f32[]{:T(128)} all-reduce(f32[]{:T(128)} %psum.35), channel_id=1, replica_groups=mesh['batch_0'=2,'batch_1'=4,'batch_2'=8,'batch_3'=2,'rep'=2] {'batch_1'}, use_global_device_ids=true, to_apply=%region_6.7 | all-reduce | flops 1 | bytes 8 | tf_op jit(solution)/shard_map/psum | solution.py:76
  254.7 13.1 %psum.37 = f32[]{:T(128)} all-reduce(f32[]{:T(128)} %psum.36), channel_id=1, replica_groups=mesh['batch_0'=2,'batch_1'=4,'batch_2'=8,'batch_3'=2,'rep'=2] {'batch_2'}, use_global_device_ids=true, to_apply=%region_7.8 | all-reduce | flops 1 | bytes 8 | tf_op jit(solution)/shard_map/psum | solution.py:76
  267.8 9.0 %psum.38 = f32[]{:T(128)} all-reduce(f32[]{:T(128)} %psum.37), channel_id=1, replica_groups=mesh['batch_0'=2,'batch_1'=4,'batch_2'=8,'batch_3'=2,'rep'=2] {'batch_3'}, use_global_device_ids=true, to_apply=%region_8.9 | all-reduce | flops 1 | bytes 8 | tf_op jit(solution)/shard_map/psum | solution.py:76
  276.9 11.5 %fusion.14 = f32[128,1024]{1,0:T(8,128)} fusion(bf16[8192,1024]{1,0:T(8,128)(2,1)} %all-gather.12.cloned.1.call-done, f32[128,8192]{1,0:T(8,128)} %get-tuple-element.19, s32[8192]{0:T(1024)S(1)} %iota_subtract_fusion, f32[8192]{0:T(1024)S(1)} %log_add_fusion, f32[128]{0:T(128)S(1)} %log_add_fusion.1, s32[128]{0:T(128)S(1)} %iota_subtract_fusion.1, ...), kind=kOutput, calls=%fused_computation.22 | convolution fusion | flops 2157051904 | bytes 21578756 | tf_op jit(solution)/shard_map/dot_general | solution.py:135
  288.4 3.5 all-to-all-start.1
  291.9 15.4 %psum.39 = f32[]{:T(128)} all-reduce(f32[]{:T(128)} %psum.38), channel_id=1, replica_groups=mesh['batch_0'=2,'batch_1'=4,'batch_2'=8,'batch_3'=2,'rep'=2] {'rep'}, use_global_device_ids=true, to_apply=%region_9.10 | all-reduce | flops 1 | bytes 8 | tf_op jit(solution)/shard_map/psum | solution.py:76
  308.0 179.3 %all-gather.8 = f32[128,1,128]{2,1,0:T(1,128)S(1)} all-gather(f32[1,1,128]{2,1,0:T(1,128)S(1)} %fusion.83), channel_id=1, replica_groups=mesh['batch_0'=2,'batch_1'=4,'batch_2'=8,'batch_3'=2,'rep'=2] {'batch_0'..., dimensions={0}, use_global_device_ids=true | all-gather | bytes 66048 | tf_op jit(solution)/shard_map/all_gather | solution.py:138
  487.2 0.7 reduce_sum.39
  488.0 31.9 %fusion.15 = f32[64,1024]{1,0:T(8,128)} fusion(bf16[16384,1024]{1,0:T(8,128)(2,1)} %all-gather.14.cloned.1.call-done, bf16[64,1024]{1,0:T(8,128)(2,1)S(1)} %copy-done, s32[64]{0:T(128)S(1)} %iota_add_fusion, f32[16384]{0:T(1024)S(1)} %bitcast.318, f32[64]{0:T(128)S(1)} %get-tuple-element.8, f32[]{:T(128)} %bitcast.317, f32[]{:T(128)S(6)} %mul.358), kind=kOutput, calls=%fused_computation.23 | convolution fusion | flops 4303421440 | bytes 34013704 | tf_op jit(solution)/shard_map/dot_general | solution.py:152
  (16 shorter events, 0.2 us)
Async XLA Ops:
  7.2 159.9 %all-gather.12.cloned.1.call-start = ((), (), s32[]{:S(2)}) async-start(), calls=%async_computation.2 | async-start | bytes 16908288 | tf_op jit(solution)/shard_map/all_gather | solution.py:106
  7.9 480.1 %all-gather.14.cloned.1.call-start = ((), (), s32[]{:S(2)}) async-start(), calls=%async_computation.3 | async-start | bytes 33816576 | tf_op jit(solution)/shard_map/all_gather | solution.py:140
  184.8 53.7 %all-to-all-start = ((f32[2,2,128]{2,1,0:T(2,128)}), f32[2,2,128]{2,1,0:T(2,128)S(1)}, u32[]{:S(2)}, u32[]{:S(2)}) async-start(f32[2,2,128]{2,1,0:T(2,128)} %broadcast_in_dim.4), calls=%async_computation | async-start | bytes 4096 | tf_op jit(solution)/shard_map/all_to_all | solution.py:14
  276.9 211.1 %copy-start = (bf16[64,1024]{1,0:T(8,128)(2,1)S(1)}, bf16[64,1024]{1,0:T(8,128)(2,1)}, u32[]{:S(2)}) copy-start(bf16[64,1024]{1,0:T(8,128)(2,1)} %param.4) | copy-start | bytes 393220
  288.4 198.9 %all-to-all-start.1 = ((f32[2,64,1024]{2,1,0:T(8,128)}), f32[2,64,1024]{2,1,0:T(8,128)S(1)}, u32[]{:S(2)}, u32[]{:S(2)}) async-start(f32[2,64,1024]{2,1,0:T(8,128)} %bitcast.46), calls=%async_computation.1 | async-start | bytes 1048576 | tf_op jit(solution)/shard_map/all_to_all | solution.py:87
Sparse Core Ops, SparseCore 0:
  11.6 155.4 all-gather.11
  170.7 214.5 all-gather.13
where the time goes:
time: 528 us
  blocking collectives  280 us (53%)
  waiting for transfers between devices  159 us (30%)
  matrix products  56.9 us (11%)
  between operations  16.6 us (3%)
  starting transfers between devices  6.79 us (1%)
  other arithmetic  6.55 us (1%)
    all_gather x1, blocking collectives, body(): all_rows_lse = lax.all_gather(row_lse, BATCH, axis=0, tiled=True)  179 us
    all_gather x1, waiting for transfers between devices, body(): whole_text = lax.all_gather(text_embed, BATCH, axis=0, tiled=True)  158 us
    psum x5, blocking collectives, over_axes(): return functools.reduce(lax.psum, axes, array)  53 us
    all_gather x4, blocking collectives, collected_together(): both, at, found = (lax.all_gather(jnp.concatenate(lines), axis), 0, {})  47.2 us
    dot_general x1, matrix products, body(): jnp.dot(weights_block, fragment, preferred_element_type=jnp.float32)  31.9 us
    dot_general x1, matrix products, body(): lax.dot_general(image_embed, whole_text, (((1,), (1,)), ((), ())), prefer...  13.5 us
    dot_general x1, matrix products, body(): jnp.dot(weights, whole_text, preferred_element_type=jnp.float32)  11.5 us
  transfers between devices with their start and end apart: 4, of which 1 were waited for; matrix products, arithmetic and copies ran while one was open for 6% of the time, Pallas kernels for 0%

commit v1 on v0

--- a/solution.py
+++ b/solution.py
@@ -4,6 +4,7 @@
 from jax import lax
 from jax.sharding import Mesh
 from jax.sharding import PartitionSpec as P
+from jax.lax import all_to_all, axis_size
 
 BATCH = ("batch_0", "batch_1", "batch_2", "batch_3")
 BATCH_REP = ("batch_0", "batch_1", "batch_2", "batch_3", "rep")
@@ -103,7 +104,10 @@
     batch_count = lax.axis_size(BATCH)
     batch_index = lax.axis_index(BATCH)
     rep_index = lax.axis_index("rep")
-    whole_text = lax.all_gather(text_embed, BATCH, axis=0, tiled=True)
+    whole_text = jnp.concatenate(
+        all_to_all(jnp.stack([text_embed for _ in range(axis_size(BATCH))], axis=0), BATCH, 0, 0),
+        axis=0,
+    )
     scores = scale_value * lax.dot_general(
         image_embed, whole_text, (((1,), (1,)), ((), ())), preferred_element_type=jnp.float32
     )

time: 528 us -> 836 us (1.58)
  waiting for transfers between devices: 159 us -> 451 us
  starting transfers between devices: 6.79 us -> 23.7 us
    all_to_all x0 -> x1, waiting for transfers between devices: none -> 450 us  [body(): all_to_all(jnp.stack([text_embed for _ in range(axis_size(BATCH))], axis=...]
    all_gather x1 -> x0, waiting for transfers between devices: 158 us -> none  [body(): whole_text = lax.all_gather(text_embed, BATCH, axis=0, tiled=True)]
    all_to_all x0 -> x1, starting transfers between devices: none -> 17 us  [body(): all_to_all(jnp.stack([text_embed for _ in range(axis_size(BATCH))], axis=...]
  transfers between devices with their start and end apart: 4 -> 4, of which waited for: 1 -> 1; matrix products, arithmetic and copies ran while one was open for 6% -> 5% of each run, Pallas kernels for 0% -> 0%
where the time goes in v1:
time: 836 us; the launch traced here: 835 us
  waiting for transfers between devices  451 us (54%)
  blocking collectives  272 us (33%)
  matrix products  56.8 us (7%)
  starting transfers between devices  23.7 us (3%)
  between operations  16.6 us (2%)
  local copies, waits for them, and re-layouts  9.04 us (1%)
    all_to_all x1, waiting for transfers between devices, body(): all_to_all(jnp.stack([text_embed for _ in range(axis_size(BATCH))], axis=...  450 us
    all_gather x1, blocking collectives, body(): all_rows_lse = lax.all_gather(row_lse, BATCH, axis=0, tiled=True)  178 us
    all_gather x4, blocking collectives, collected_together(): both, at, found = (lax.all_gather(jnp.concatenate(lines), axis), 0, {})  48.4 us
    psum x5, blocking collectives, over_axes(): return functools.reduce(lax.psum, axes, array)  45.6 us
    dot_general x1, matrix products, body(): jnp.dot(weights_block, fragment, preferred_element_type=jnp.float32)  31.9 us
    all_to_all x1, starting transfers between devices, body(): all_to_all(jnp.stack([text_embed for _ in range(axis_size(BATCH))], axis=...  17 us
  transfers between devices with their start and end apart: 4, of which 1 were waited for; matrix products, arithmetic and copies ran while one was open for 5% of the time, Pallas kernels for 0%

profile of v1, /device:TPU:1, one launch (start us, length us, event | category | flops | bytes accessed | tf_op | source)
XLA Modules:
  0.0 835.2 jit_solution(7280267484479434481)
XLA Ops:
  7.2 0.7 all-gather.11.cloned.1.call-update
  7.9 6.7 stack.2
  14.6 17.0 %all-to-all-start = ((bf16[128,64,1024]{2,1,0:T(8,128)(2,1)}), bf16[128,64,1024]{2,1,0:T(8,128)(2,1)}, u32[]{:S(2)}, u32[]{:S(2)}) async-start(bf16[128,64,1024]{2,1,0:T(8,128)(2,1)} %stack.2), calls=%async_computation | async-start | bytes 33554432 | tf_op jit(solution)/shard_map/all_to_all | solution.py:108
  32.3 450.0 %all-to-all-done = bf16[128,64,1024]{2,1,0:T(8,128)(2,1)} async-done(((bf16[128,64,1024]{2,1,0:T(8,128)(2,1)}), bf16[128,64,1024]{2,1,0:T(8,128)(2,1)}, u32[]{:S(2)}, u32[]{:S(2)}) %all-to-all-start) | async-done | bytes 16777248 | tf_op jit(solution)/shard_map/all_to_all | solution.py:108
  482.3 13.4 %fusion.72 = (f32[128]{0:T(128)S(1)}, f32[8192]{0:T(1024)S(1)}, f32[128,8192]{1,0:T(8,128)}) fusion(bf16[128,1024]{1,0:T(8,128)(2,1)S(1)} %copy-done, bf16[8192,1024]{1,0:T(8,128)(2,1)} %bitcast.1, f32[]{:T(128)} %bitcast.316), kind=kOutput, calls=%fused_computation.126 | convolution fusion | flops 2150621184 | bytes 21266948 | tf_op jit(solution)/shard_map/dot_general | solution.py:111
  495.7 3.5 exponential_reduce_fusion.1
  499.2 0.6 broadcast_in_dim.4
  499.8 3.2 all-to-all-start.1
  503.0 0.1 maximum_bitcast_fusion
  503.1 5.3 all-gather.4
  508.4 0.1 fusion.47
  508.5 0.1 maximum_bitcast_fusion.1
  508.6 9.8 %all-gather.5 = f32[4,2,8192]{2,1,0:T(2,128)S(1)} all-gather(f32[1,2,8192]{2,1,0:T(2,128)S(1)} %maximum_bitcast_fusion.1), channel_id=3, replica_groups=mesh['batch_0'=2,'batch_1'=4,'batch_2'=8,'batch_3'=2,'rep'=2] {'batch_1'}, dimensions={0}, use_global_device_ids=true | all-gather | bytes 327680 | tf_op jit(solution)/shard_map/all_gather | solution.py:58
  518.4 0.3 fusion.38
  518.7 0.1 maximum_bitcast_fusion.2
  518.8 21.6 %all-gather.6 = f32[8,2,8192]{2,1,0:T(2,128)S(1)} all-gather(f32[1,2,8192]{2,1,0:T(2,128)S(1)} %maximum_bitcast_fusion.2), channel_id=4, replica_groups=mesh['batch_0'=2,'batch_1'=4,'batch_2'=8,'batch_3'=2,'rep'=2] {'batch_2'}, dimensions={0}, use_global_device_ids=true | all-gather | bytes 589824 | tf_op jit(solution)/shard_map/all_gather | solution.py:58
  540.4 0.7 fusion.17
  541.2 11.7 %all-gather.7 = f32[2,2,8192]{2,1,0:T(2,128)S(1)} all-gather(f32[1,2,8192]{2,1,0:T(2,128)S(1)} %maximum_bitcast_fusion.3), channel_id=5, replica_groups=mesh['batch_0'=2,'batch_1'=4,'batch_2'=8,'batch_3'=2,'rep'=2] {'batch_3'}, dimensions={0}, use_global_device_ids=true | all-gather | bytes 196608 | tf_op jit(solution)/shard_map/all_gather | solution.py:58
  552.9 0.1 fusion.76
  553.0 0.8 dynamic_slice.11
  553.9 0.8 gather_fusion
  554.7 0.7 subtract_reduce_fusion
  555.4 5.9 psum.35
  561.3 6.6 psum.36
  567.9 14.8 %psum.37 = f32[]{:T(128)} all-reduce(f32[]{:T(128)} %psum.36), channel_id=1, replica_groups=mesh['batch_0'=2,'batch_1'=4,'batch_2'=8,'batch_3'=2,'rep'=2] {'batch_2'}, use_global_device_ids=true, to_apply=%region_7.8 | all-reduce | flops 1 | bytes 8 | tf_op jit(solution)/shard_map/psum | solution.py:77
  582.7 9.6 %psum.38 = f32[]{:T(128)} all-reduce(f32[]{:T(128)} %psum.37), channel_id=1, replica_groups=mesh['batch_0'=2,'batch_1'=4,'batch_2'=8,'batch_3'=2,'rep'=2] {'batch_3'}, use_global_device_ids=true, to_apply=%region_8.9 | all-reduce | flops 1 | bytes 8 | tf_op jit(solution)/shard_map/psum | solution.py:77
  592.3 11.5 %fusion.14 = f32[128,1024]{1,0:T(8,128)} fusion(bf16[8192,1024]{1,0:T(8,128)(2,1)} %bitcast.1, f32[128,8192]{1,0:T(8,128)} %get-tuple-element.19, s32[8192]{0:T(1024)S(1)} %iota_subtract_fusion, f32[8192]{0:T(1024)S(1)} %log_add_fusion, f32[128]{0:T(128)S(1)} %log_add_fusion.1, s32[128]{0:T(128)S(1)} %iota_subtract_fusion.1, ...), kind=kOutput, calls=%fused_computation.22 | convolution fusion | flops 2157051904 | bytes 21578756 | tf_op jit(solution)/shard_map/dot_general | solution.py:139
  603.8 3.5 all-to-all-start.2
  607.3 8.7 %psum.39 = f32[]{:T(128)} all-reduce(f32[]{:T(128)} %psum.38), channel_id=1, replica_groups=mesh['batch_0'=2,'batch_1'=4,'batch_2'=8,'batch_3'=2,'rep'=2] {'rep'}, use_global_device_ids=true, to_apply=%region_9.10 | all-reduce | flops 1 | bytes 8 | tf_op jit(solution)/shard_map/psum | solution.py:77
  616.7 177.9 %all-gather.8 = f32[128,1,128]{2,1,0:T(1,128)S(1)} all-gather(f32[1,1,128]{2,1,0:T(1,128)S(1)} %fusion.83), channel_id=1, replica_groups=mesh['batch_0'=2,'batch_1'=4,'batch_2'=8,'batch_3'=2,'rep'=2] {'batch_0'..., dimensions={0}, use_global_device_ids=true | all-gather | bytes 66048 | tf_op jit(solution)/shard_map/all_gather | solution.py:142
  794.6 0.7 reduce_sum.39
  795.4 31.9 %fusion.15 = f32[64,1024]{1,0:T(8,128)} fusion(bf16[16384,1024]{1,0:T(8,128)(2,1)} %all-gather.11.cloned.1.call-done, bf16[64,1024]{1,0:T(8,128)(2,1)S(1)} %copy-done.1, s32[64]{0:T(128)S(1)} %iota_add_fusion, f32[16384]{0:T(1024)S(1)} %bitcast.319, f32[64]{0:T(128)S(1)} %get-tuple-element.8, f32[]{:T(128)} %bitcast.318, f32[]{:T(128)S(6)} %mul.358), kind=kOutput, calls=%fused_computation.23 | convolution fusion | flops 4303421440 | bytes 34013704 | tf_op jit(solution)/shard_map/dot_general | solution.py:156
  (18 shorter events, 0.2 us)
Async XLA Ops:
  7.2 788.2 %all-gather.11.cloned.1.call-start = ((), (), s32[]{:S(2)}) async-start(), calls=%async_computation.3 | async-start | bytes 33816576 | tf_op jit(solution)/shard_map/all_gather | solution.py:144
  14.6 467.7 %copy-start = (bf16[128,1024]{1,0:T(8,128)(2,1)S(1)}, bf16[128,1024]{1,0:T(8,128)(2,1)}, u32[]{:S(2)}) copy-start(bf16[128,1024]{1,0:T(8,128)(2,1)} %param.3) | copy-start | bytes 786436
  14.6 467.7 %all-to-all-start = ((bf16[128,64,1024]{2,1,0:T(8,128)(2,1)}), bf16[128,64,1024]{2,1,0:T(8,128)(2,1)}, u32[]{:S(2)}, u32[]{:S(2)}) async-start(bf16[128,64,1024]{2,1,0:T(8,128)(2,1)} %stack.2), calls=%async_computation | async-start | bytes 33554432 | tf_op jit(solution)/shard_map/all_to_all | solution.py:108
  499.8 54.9 %all-to-all-start.1 = ((f32[2,2,128]{2,1,0:T(2,128)}), f32[2,2,128]{2,1,0:T(2,128)S(1)}, u32[]{:S(2)}, u32[]{:S(2)}) async-start(f32[2,2,128]{2,1,0:T(2,128)} %broadcast_in_dim.4), calls=%async_computation.1 | async-start | bytes 4096 | tf_op jit(solution)/shard_map/all_to_all | solution.py:15
  592.3 203.1 %copy-start.1 = (bf16[64,1024]{1,0:T(8,128)(2,1)S(1)}, bf16[64,1024]{1,0:T(8,128)(2,1)}, u32[]{:S(2)}) copy-start(bf16[64,1024]{1,0:T(8,128)(2,1)} %param.4) | copy-start | bytes 393220
  603.8 190.9 %all-to-all-start.2 = ((f32[2,64,1024]{2,1,0:T(8,128)}), f32[2,64,1024]{2,1,0:T(8,128)S(1)}, u32[]{:S(2)}, u32[]{:S(2)}) async-start(f32[2,64,1024]{2,1,0:T(8,128)} %bitcast.47), calls=%async_computation.2 | async-start | bytes 1048576 | tf_op jit(solution)/shard_map/all_to_all | solution.py:88
Sparse Core Ops, SparseCore 0:
  11.6 454.2 all-gather.10
